TPU v7x, 32 devices: a whole 2x2x4 slice. The times are simulated.
32 devices in a mesh: dp: 8 (over z, x), tensor: 4 (over y, core).
Axes of the slice: x: 2, y: 2, z: 4, core: 2. Of those that a mesh axis runs over, the one named last changes fastest.
Arguments:
- tokens: bfloat16 [64, 258, 768], P('dp'), may hold values from -6 to 6
- metadata: int32 [64], P('dp'), may hold values 0 or 1
- cotangent: bfloat16 [64, 258, 768], P('dp'), may hold values from -6 to 6
- w_query: bfloat16 [768, 768], P(None, 'tensor'), may hold values from -0.21875 to 0.21875
- w_key: bfloat16 [768, 768], P(None, 'tensor'), may hold values from -0.21875 to 0.21875
- w_value: bfloat16 [768, 768], P(None, 'tensor'), may hold values from -0.21875 to 0.21875
- w_out: bfloat16 [768, 768], P('tensor'), may hold values from -1.75 to 1.75
- b_query: float32 [768], P('tensor'), may hold values from -1.5 to 1.5
- b_value: float32 [768], P('tensor'), may hold values from -1.5 to 1.5
- b_out: float32 [768], replicated, may hold values from -1.5 to 1.5
- w_up: bfloat16 [768, 3072], P(None, 'tensor'), may hold values from -0.21875 to 0.21875
- b_up: float32 [3072], P('tensor'), may hold values from -1.5 to 1.5
- w_down: bfloat16 [3072, 768], P('tensor'), may hold values from -0.21875 to 0.21875
- b_down: float32 [768], replicated, may hold values from -1.5 to 1.5
- gain_one: float32 [768], replicated, may hold values from 0.25 to 1.75
- shift_one: float32 [768], replicated, may hold values from -1.5 to 1.5
- gain_two: float32 [768], replicated, may hold values from 0.25 to 1.75
- shift_two: float32 [768], replicated, may hold values from -1.5 to 1.5
Outputs:
- layer_out: bfloat16 [64, 258, 768], P('dp')
- grad_tokens: float32 [64, 258, 768], P('dp')
- grad_w_query: float32 [768, 768], P(None, 'tensor')
- grad_w_key: float32 [768, 768], P(None, 'tensor')
- grad_w_value: float32 [768, 768], P(None, 'tensor')
- grad_w_out: float32 [768, 768], P('tensor')
- grad_b_query: float32 [768], P('tensor')
- grad_b_value: float32 [768], P('tensor')
- grad_b_out: float32 [768], replicated
- grad_w_up: float32 [768, 3072], P(None, 'tensor')
- grad_b_up: float32 [3072], P('tensor')
- grad_w_down: float32 [3072, 768], P('tensor')
- grad_b_down: float32 [768], replicated
- grad_gain_one: float32 [768], replicated
- grad_shift_one: float32 [768], replicated
- grad_gain_two: float32 [768], replicated
- grad_shift_two: float32 [768], replicated
All inputs are finite; a program needn't handle non-finite values. No bound on the sum of `metadata` on one device may be relied on, other than what follows from the above.
Results may differ from a plain program's by a relative error of at most 0.012.
Values sent between devices are 32-bit elements; how exact they have to be, the bound alone decides.
A program may use at most 192 MiB of HBM per device.

v0:
```python
import math
import jax
import jax.numpy as jnp
from jax import lax
from jax.sharding import PartitionSpec as P

HEAD_DIM = 64
NORM_EPSILON = 1e-05


def layer_norm(source_tokens, gain, shift):
    average = jnp.mean(source_tokens, -1, keepdims=True)
    mean_removed = source_tokens - average
    variance = jnp.mean(mean_removed * mean_removed, -1, keepdims=True)
    return mean_removed * lax.rsqrt(variance + NORM_EPSILON) * gain + shift


def gelu_exact(source_tokens):
    return jax.nn.gelu(source_tokens, approximate=False)


def multiply(left_mat, right_mat):
    return jnp.dot(left_mat, right_mat, preferred_element_type=jnp.float32)


def contract_rows(left_mat, right_mat):
    return lax.dot_general(
        left_mat, right_mat, (((0,), (0,)), ((), ())), preferred_element_type=jnp.float32
    )


def contract_cols(left_mat, right_mat):
    return lax.dot_general(
        left_mat, right_mat, (((1,), (1,)), ((), ())), preferred_element_type=jnp.float32
    )


def column_sums(matrix):
    return jnp.sum(matrix.astype(jnp.float32), 0)


def shards(
    tokens,
    metadata,
    cotangent,
    w_query,
    w_key,
    w_value,
    w_out,
    b_query,
    b_value,
    b_out,
    w_up,
    b_up,
    w_down,
    b_down,
    gain_one,
    shift_one,
    gain_two,
    shift_two,
):
    samples, length, model_width = tokens.shape
    row_count = samples * length
    local_width = w_query.shape[1]
    local_heads = local_width // HEAD_DIM
    score_scale = 1.0 / math.sqrt(HEAD_DIM)
    position = lax.broadcasted_iota(jnp.int32, (samples, length), 1)
    keep_mask = jnp.where(
        position == 1, metadata[:, None].astype(jnp.float32), jnp.float32(1.0)
    ).reshape(row_count, 1)
    inputs = tokens.reshape(row_count, model_width).astype(jnp.float32) * keep_mask

    def split_heads(matrix):
        return matrix.reshape(samples, length, local_heads, HEAD_DIM)

    normed, first_norm_backward = jax.vjp(layer_norm, inputs, gain_one, shift_one)
    normed_low = normed.astype(jnp.bfloat16)
    queries = (multiply(normed_low, w_query) + b_query).astype(jnp.bfloat16)
    key_rows = multiply(normed_low, w_key).astype(jnp.bfloat16)
    values = (multiply(normed_low, w_value) + b_value).astype(jnp.bfloat16)
    head_queries = split_heads(queries)
    head_keys = split_heads(key_rows)
    head_values = split_heads(values)
    scores = (
        jnp.einsum("sqhc,skhc->shqk", head_queries, head_keys, preferred_element_type=jnp.float32)
        * score_scale
    )
    row_max = jnp.max(scores, -1, keepdims=True)
    row_total = jnp.sum(jnp.exp(scores - row_max), -1, keepdims=True)
    logsum = row_max + jnp.log(row_total)
    probs_low = jnp.exp(scores - logsum).astype(jnp.bfloat16)
    mixture = jnp.einsum(
        "shqk,skhc->sqhc", probs_low, head_values, preferred_element_type=jnp.float32
    )
    mixture = mixture.reshape(row_count, local_width).astype(jnp.bfloat16)
    branch = lax.psum(multiply(mixture, w_out), "tensor") + b_out
    middle = inputs + branch
    normed_two, norm_two_back = jax.vjp(layer_norm, middle, gain_two, shift_two)
    normed_two_low = normed_two.astype(jnp.bfloat16)
    hidden = multiply(normed_two_low, w_up) + b_up
    active, gelu_back = jax.vjp(gelu_exact, hidden)
    active_reduced = active.astype(jnp.bfloat16)
    branch_two = lax.psum(multiply(active_reduced, w_down), "tensor") + b_down
    layer_out = (middle + branch_two).astype(jnp.bfloat16).reshape(samples, length, model_width)
    grad_out = cotangent.reshape(row_count, model_width).astype(jnp.float32)
    grad_out_low = grad_out.astype(jnp.bfloat16)
    grad_b_down = column_sums(grad_out_low)
    grad_w_down = contract_rows(active_reduced, grad_out_low)
    grad_active = contract_cols(grad_out_low, w_down)
    grad_hidden = gelu_back(grad_active)[0].astype(jnp.bfloat16)
    grad_b_up = column_sums(grad_hidden)
    grad_w_up = contract_rows(normed_two_low, grad_hidden)
    grad_normed_two = lax.psum(contract_cols(grad_hidden, w_up), "tensor")
    grad_mid_part, grad_gain_two, grad_shift_two = norm_two_back(grad_normed_two)
    grad_middle = grad_out + grad_mid_part
    mlp_group = (grad_w_up, grad_b_up, grad_w_down, grad_b_down, grad_gain_two, grad_shift_two)
    grad_mid_low = grad_middle.astype(jnp.bfloat16)
    grad_b_out = column_sums(grad_mid_low)
    grad_w_out = contract_rows(mixture, grad_mid_low)
    grad_mixture = split_heads(contract_cols(grad_mid_low, w_out).astype(jnp.bfloat16))
    scores_again = (
        jnp.einsum("sqhc,skhc->shqk", head_queries, head_keys, preferred_element_type=jnp.float32)
        * score_scale
    )
    attn_probs = jnp.exp(scores_again - logsum)
    probs_again = attn_probs.astype(jnp.bfloat16)
    grad_values = jnp.einsum(
        "shqk,sqhc->skhc", probs_again, grad_mixture, preferred_element_type=jnp.float32
    )
    grad_values = grad_values.reshape(row_count, local_width).astype(jnp.bfloat16)
    grad_probs = jnp.einsum(
        "sqhc,skhc->shqk", grad_mixture, head_values, preferred_element_type=jnp.float32
    )
    grad_scores = attn_probs * (grad_probs - jnp.sum(attn_probs * grad_probs, -1, keepdims=True))
    grad_scores = grad_scores.astype(jnp.bfloat16)
    grad_queries = (
        jnp.einsum("shqk,skhc->sqhc", grad_scores, head_keys, preferred_element_type=jnp.float32)
        * score_scale
    )
    grad_queries = grad_queries.reshape(row_count, local_width).astype(jnp.bfloat16)
    grad_keys = (
        jnp.einsum("shqk,sqhc->skhc", grad_scores, head_queries, preferred_element_type=jnp.float32)
        * score_scale
    )
    grad_keys = grad_keys.reshape(row_count, local_width).astype(jnp.bfloat16)
    grad_w_query = contract_rows(normed_low, grad_queries)
    grad_w_key = contract_rows(normed_low, grad_keys)
    grad_w_value = contract_rows(normed_low, grad_values)
    grad_b_query = column_sums(grad_queries)
    grad_b_value = column_sums(grad_values)
    grad_normalized_piece = (
        contract_cols(grad_queries, w_query)
        + contract_cols(grad_keys, w_key)
        + contract_cols(grad_values, w_value)
    )
    grad_normed = lax.psum(grad_normalized_piece, "tensor")
    grad_in_part, grad_gain_one, grad_shift_one = first_norm_backward(grad_normed)
    grad_tokens = ((grad_middle + grad_in_part) * keep_mask).reshape(samples, length, model_width)
    attn_group = (
        grad_w_query,
        grad_w_key,
        grad_w_value,
        grad_w_out,
        grad_b_query,
        grad_b_value,
        grad_b_out,
        grad_gain_one,
        grad_shift_one,
    )
    summed = lax.psum(mlp_group + attn_group, "dp")
    mlp_group = summed[:6]
    attn_group = summed[6:]
    return (
        layer_out,
        grad_tokens,
        attn_group[0],
        attn_group[1],
        attn_group[2],
        attn_group[3],
        attn_group[4],
        attn_group[5],
        attn_group[6],
        mlp_group[0],
        mlp_group[1],
        mlp_group[2],
        mlp_group[3],
        attn_group[7],
        attn_group[8],
        mlp_group[4],
        mlp_group[5],
    )


def solution(mesh):
    return jax.shard_map(
        shards,
        mesh=mesh,
        in_specs=(
            P("dp", None, None),
            P("dp"),
            P("dp", None, None),
            P(None, "tensor"),
            P(None, "tensor"),
            P(None, "tensor"),
            P("tensor", None),
            P("tensor"),
            P("tensor"),
            P(),
            P(None, "tensor"),
            P("tensor"),
            P("tensor", None),
            P(),
            P(),
            P(),
            P(),
            P(),
        ),
        out_specs=(
            P("dp", None, None),
            P("dp", None, None),
            P(None, "tensor"),
            P(None, "tensor"),
            P(None, "tensor"),
            P("tensor", None),
            P("tensor"),
            P("tensor"),
            P(),
            P(None, "tensor"),
            P("tensor"),
            P("tensor", None),
            P(),
            P(),
            P(),
            P(),
            P(),
        ),
        check_vma=False,
    )
```

profile of v0, /device:TPU:0, one launch (start us, length us, event | category | flops | bytes accessed | tf_op | source)
XLA Modules:
  0.0 897.8 jit_solution(9342128070286131994)
XLA Ops:
  11.4 5.4 copy.99
  19.3 5.0 reshape.276
  38.4 4.0 fusion.9
  59.2 4.2 copy.109
  63.5 3.7 reshape.273
  67.2 115.4 %all-reduce.8.cloned.1.call-done = f32[2064,768]{1,0:T(8,128)} async-done(((f32[2064,768]{1,0:T(8,128)}), f32[2064,768]{1,0:T(8,128)}) %all-reduce.8.cloned.1.call-update) | async-done | bytes 6340624 | tf_op jit(solution)/shard_map/psum | solution.py:96
  182.6 5.8 fusion.34
  194.6 18.7 %convert_reduce_fusion.1 = (f32[768]{0:T(1024)}, bf16[2064,768]{1,0:T(8,128)(2,1)S(1)}, f32[2064,768]{1,0:T(8,128)}) fusion(f32[2064,768]{1,0:T(8,128)S(1)} %convolution_add_fusion, bf16[2064,768]{1,0:T(8,128)(2,1)S(1)} %copy-done.8, bf16[768,768]{1,0:T(8,128)(2,1)S(1)} %copy-done), kind=kOutput, calls=%fused_computation.12 | convolution fusion | flops 2552093952 | bytes 20204544 | tf_op jit(solution)/shard_map/dot_general | solution.py:33
  215.0 4.6 fusion.37
  219.7 5.5 multiply_convert_fusion.1
  226.9 4.8 fusion.36
  231.6 108.8 %all-reduce.10.cloned.1.call-done = f32[2064,768]{1,0:T(8,128)} async-done(((f32[2064,768]{1,0:T(8,128)}), f32[2064,768]{1,0:T(8,128)}) %all-reduce.10.cloned.1.call-update) | async-done | bytes 6340624 | tf_op jit(solution)/shard_map/psum | solution.py:113
  340.5 6.5 multiply_reduce_fusion.2
  347.0 6.8 fusion.33
  360.8 6.8 convert_reduce_fusion.3
  367.6 7.8 multiply_reduce_fusion
  375.5 10.9 %multiply_convert_fusion = bf16[8,3,258,258]{2,3,1,0:T(8,128)(2,1)} fusion(f32[8,3,258,258]{2,3,1,0:T(8,128)} %get-tuple-element.124, f32[8,3,258,258]{2,3,1,0:T(8,128)} %copy-done.2, f32[8,3,258]{2,1,0:T(4,128)S(1)} %get-tuple-element.123, f32[8,3,258]{2,1,0:T(4,128)S(1)} %log_add_fusion), kind=kLoop, calls=%fused_computation | loop fusion | flops 7987680 | bytes 16024896 | tf_op jit(solution)/shard_map/convert_element_type | solution.py:135
  386.4 5.5 fusion.13
  408.4 3.7 add_add_fusion.2
  422.6 7.4 fusion.41
  430.0 4.4 fusion.42
  443.9 191.5 %all-reduce.14.cloned.1.call-done = (f32[2064,768]{1,0:T(8,128)}, f32[2064,768]{1,0:T(8,128)}) async-done(((f32[2064,768]{1,0:T(8,128)}, f32[2064,768]{1,0:T(8,128)}), (f32[2064,768]{1,0:T(8,128)}, f32[2064,768]{1,0:T(8,128)})) %all-reduce.14.cloned.1.call-update) | async-done | bytes 12681232 | tf_op jit(solution)/shard_map/psum | solution.py:103
  635.5 7.2 add_convert_fusion.2
  642.7 3.8 reshape.272
  646.5 5.0 copy.123
  651.5 7.1 multiply_reduce_fusion.3
  658.7 7.8 fusion.32
  666.5 7.5 add_multiply_fusion
  674.0 5.1 reshape.275
  679.1 7.7 copy.124
  686.8 39.8 %all-reduce = (f32[192]{0:T(256)}, f32[192]{0:T(256)}, f32[768]{0:T(1024)}, f32[768]{0:T(1024)}, f32[768]{0:T(1024)}, /*index=5*/f32[768]{0:T(1024)}, f32[768]{0:T(1024)}, f32[768]{0:T(1024)}, f32[768]{0:T(1024)}) all-reduce(f32[192]{0:T(256)S(1)} %reduce_sum.218, ...), channel_id=1, replica_groups=mesh['dp'=8,'tensor'=4] {'dp'}, use_global_device_ids=true, to_apply=%region_20.21 | all-reduce | flops 5760 | bytes 46080 | tf_op jit(solution)/shard_map/psum | solution.py:170
  726.6 153.7 %all-reduce.12.cloned.1.call-done = (f32[768,192]{0,1:T(8,128)}, f32[768,192]{0,1:T(8,128)}, f32[768,192]{0,1:T(8,128)}, f32[192,768]{1,0:T(8,128)}, f32[768,768]{1,0:T(8,128)}, /*index=5*/f32[768,768]{1,0:T(8,128)}) async-done(((f32[768,192]{0,1:T(8,128)}, f32[768,192]{0,1:T(8,128)}, f32[768,192]{0,1:T(8,128)}, f32[192,768]{1,0:T(8,128)}, f32[768,768]{1,0:T(8,128)}, /*index=5*/f32[768,768]{1,0:T(8,128)}), ...) | async-done | bytes 7077904 | tf_op jit(solution)/shard_map/psum | solution.py:170
  (211 shorter events, 100.9 us)
Async XLA Ops:
  7.2 187.1 %copy-start = (bf16[768,768]{1,0:T(8,128)(2,1)S(1)}, bf16[768,768]{1,0:T(8,128)(2,1)}, u32[]{:S(2)}) copy-start(bf16[768,768]{1,0:T(8,128)(2,1)} %param.30) | copy-start | bytes 3538948
  7.2 175.4 %all-reduce.8.cloned.1.call-start = ((), (), s32[]{:S(2)}) async-start(), calls=%async_computation | async-start | bytes 12681216 | tf_op jit(solution)/shard_map/psum | solution.py:96
  8.2 174.4 %copy-start.35 = (f32[2064]{0:T(1024)}, f32[2064]{0:T(1024)S(1)}, u32[]{:S(2)}) copy-start(f32[2064]{0:T(1024)S(1)} %select_n.13) | copy-start | bytes 24772
  8.3 8.5 copy-start.31
  11.3 13.1 %copy-start.43 = (f32[2064]{0:T(1024)}, f32[2064]{0:T(1024)S(1)}, u32[]{:S(2)}) copy-start(f32[2064]{0:T(1024)S(1)} %div.39) | copy-start | bytes 24772
  31.0 7.4 copy-start.38
  31.0 7.4 copy-start.64
  32.4 13.0 %copy-start.12 = (bf16[8,258,3,64]{1,0,3,2:T(8,128)(2,1)}, bf16[8,258,3,64]{1,0,3,2:T(8,128)(2,1)S(1)}, u32[]{:S(2)}) copy-start(bf16[8,258,3,64]{1,0,3,2:T(8,128)(2,1)S(1)} %reshape.271) | copy-start | bytes 2377732
  59.2 123.4 %copy-start.57 = (f32[768]{0:T(1024)S(1)}, f32[768]{0:T(1024)}, u32[]{:S(2)}) copy-start(f32[768]{0:T(1024)} %param.27) | copy-start | bytes 9220
  59.2 281.3 %all-reduce.10.cloned.1.call-start = ((), (), s32[]{:S(2)}) async-start(), calls=%async_computation.1 | async-start | bytes 12681216 | tf_op jit(solution)/shard_map/psum | solution.py:113
  194.6 18.7 %copy-start.23 = (f32[2064,768]{1,0:T(8,128)}, f32[2064,768]{1,0:T(8,128)S(1)}, u32[]{:S(2)}) copy-start(f32[2064,768]{1,0:T(8,128)S(1)} %convolution_add_fusion) | copy-start | bytes 19021828
  219.7 415.8 %all-reduce.14.cloned.1.call-start = ((), (), s32[]{:S(2)}) async-start(), calls=%async_computation.3 | async-start | bytes 25362432 | tf_op jit(solution)/shard_map/psum | solution.py:103
  375.5 10.9 %copy-start.15 = (bf16[8,258,3,64]{1,0,3,2:T(8,128)(2,1)S(1)}, bf16[8,258,3,64]{1,0,3,2:T(8,128)(2,1)}, u32[]{:S(2)}) copy-start(bf16[8,258,3,64]{1,0,3,2:T(8,128)(2,1)} %copy-done.14) | copy-start | bytes 2377732
  393.3 13.0 %copy-start.39 = (bf16[768,192]{0,1:T(8,128)(2,1)S(1)}, bf16[768,192]{0,1:T(8,128)(2,1)}, u32[]{:S(2)}) copy-start(bf16[768,192]{0,1:T(8,128)(2,1)} %param.21) | copy-start | bytes 884740
  397.1 11.3 %copy-start.21 = (bf16[2064,192]{0,1:T(8,128)(2,1)}, bf16[2064,192]{0,1:T(8,128)(2,1)S(1)}, u32[]{:S(2)}) copy-start(bf16[2064,192]{0,1:T(8,128)(2,1)S(1)} %convert_element_type.155) | copy-start | bytes 2377732
  412.2 468.1 %all-reduce.12.cloned.1.call-start = ((), (), s32[]{:S(2)}) async-start(), calls=%async_computation.2 | async-start | bytes 14155776 | tf_op jit(solution)/shard_map/psum | solution.py:170
  422.6 7.4 copy-start.10
  422.6 7.4 copy-start.27
  439.6 195.9 %copy-start.59 = (f32[768]{0:T(1024)S(1)}, f32[768]{0:T(1024)}, u32[]{:S(2)}) copy-start(f32[768]{0:T(1024)} %param.31) | copy-start | bytes 9220
  642.7 8.8 copy-start.36
  642.7 8.8 copy-start.44
  642.7 8.8 copy-start.46
  646.5 12.2 %slice-start = ((s8[6340608]{0:T(1024)(128)(4,1)}), s8[4194304]{0:T(1024)(128)(4,1)S(1)}, s32[]{:S(2)}) async-start(s8[6340608]{0:T(1024)(128)(4,1)} %bitcast.70), calls=%async_computation.4 | async-start | bytes 8388608
  651.5 7.1 copy-start.48
  651.5 7.2 slice-start.1
  658.7 7.8 copy-start.11
  679.1 7.7 copy-start.53
  679.1 7.7 copy-start.54
  679.1 7.7 copy-start.60
  880.3 7.9 copy-start.30
  880.3 9.3 %copy-start.29 = (f32[768,768]{1,0:T(8,128)S(1)}, f32[768,768]{1,0:T(8,128)}, u32[]{:S(2)}) copy-start(f32[768,768]{1,0:T(8,128)} %get-tuple-element.140) | copy-start | bytes 7077892
  880.3 10.7 %copy-start.1 = (bf16[768,768]{1,0:T(8,128)(2,1)S(1)}, bf16[768,768]{1,0:T(8,128)(2,1)}, u32[]{:S(2)}) copy-start(bf16[768,768]{1,0:T(8,128)(2,1)} %param.30) | copy-start | bytes 3538948
  (40 other events, 132.0 us)
Sparse Core Ops, SparseCore 0:
  59.3 123.2 all-reduce.7
  219.8 120.6 all-reduce.9
  412.3 223.0 all-reduce.13
  642.3 237.8 all-reduce.11
where the time goes:
time: 906 us; the launch traced here: 898 us
  waiting for transfers between devices  569 us (63%)
  matrix products  94.5 us (10%)
  local copies, waits for them, and re-layouts  92.1 us (10%)
  other arithmetic  86.8 us (10%)
  blocking collectives  39.8 us (4%)
  between operations  14.8 us (2%)
    psum x1, waiting for transfers between devices, shards(): branch_two = lax.psum(multiply(active_reduced, w_down), 'tensor') + b_down  192 us
    psum x1, waiting for transfers between devices, shards(): summed = lax.psum(mlp_group + attn_group, 'dp')  154 us
    psum x1, waiting for transfers between devices, shards(): branch = lax.psum(multiply(mixture, w_out), 'tensor') + b_out  115 us
    psum x1, waiting for transfers between devices, shards(): grad_normed_two = lax.psum(contract_cols(grad_hidden, w_up), 'tensor')  109 us
    psum x1, blocking collectives, shards(): summed = lax.psum(mlp_group + attn_group, 'dp')  39.8 us
    unnamed x145, local copies, waits for them, and re-layouts  37 us
    dot_general x6, matrix products, contract_cols(): lax.dot_general(left_mat, right_mat, (((1,), (1,)), ((), ())), preferred_...  30.3 us
    dot_general x6, matrix products, multiply(): return jnp.dot(left_mat, right_mat, preferred_element_type=jnp.float32)  20 us
  transfers between devices with their start and end apart: 4, of which 4 were waited for; matrix products, arithmetic and copies ran while one was open for 11% of the time, Pallas kernels for 0%

commit v1 on v0

--- a/solution.py
+++ b/solution.py
@@ -93,7 +93,7 @@
         "shqk,skhc->sqhc", probs_low, head_values, preferred_element_type=jnp.float32
     )
     mixture = mixture.reshape(row_count, local_width).astype(jnp.bfloat16)
-    branch = lax.psum(multiply(mixture, w_out), "tensor") + b_out
+    branch = jnp.sum(lax.all_gather(multiply(mixture, w_out), "tensor"), axis=0) + b_out
     middle = inputs + branch
     normed_two, norm_two_back = jax.vjp(layer_norm, middle, gain_two, shift_two)
     normed_two_low = normed_two.astype(jnp.bfloat16)

time: 906 us -> 969 us (1.070)
  waiting for transfers between devices: 569 us -> 609 us
  other arithmetic: 86.8 us -> 111 us
    all_gather x0 -> x1, waiting for transfers between devices: none -> 151 us  [shards(): lax.all_gather(multiply(mixture, w_out), 'tensor')]
    psum x1 -> x0, waiting for transfers between devices: 115 us -> none  [shards(): branch = lax.psum(multiply(mixture, w_out), 'tensor') + b_out]
    reduce_sum x0 -> x1, other arithmetic: none -> 12.5 us  [shards(): jnp.sum(lax.all_gather(multiply(mixture, w_out), 'tensor'), axis=0) + b_out]
    unnamed x145 -> x141, local copies, waits for them, and re-layouts: 37 us -> 37.2 us
  transfers between devices with their start and end apart: 4 -> 4, of which waited for: 4 -> 4; matrix products, arithmetic and copies ran while one was open for 11% -> 10% of each run, Pallas kernels for 0% -> 0%
where the time goes in v1:
time: 969 us; the launch traced here: 960 us
  waiting for transfers between devices  609 us (63%)
  other arithmetic  111 us (11%)
  matrix products  94.6 us (10%)
  local copies, waits for them, and re-layouts  88.9 us (9%)
  blocking collectives  40.1 us (4%)
  between operations  15.1 us (2%)
    psum x1, waiting for transfers between devices, shards(): branch_two = lax.psum(multiply(active_reduced, w_down), 'tensor') + b_down  197 us
    psum x1, waiting for transfers between devices, shards(): summed = lax.psum(mlp_group + attn_group, 'dp')  153 us
    all_gather x1, waiting for transfers between devices, shards(): lax.all_gather(multiply(mixture, w_out), 'tensor')  151 us
    psum x1, waiting for transfers between devices, shards(): grad_normed_two = lax.psum(contract_cols(grad_hidden, w_up), 'tensor')  109 us
    psum x1, blocking collectives, shards(): summed = lax.psum(mlp_group + attn_group, 'dp')  40.1 us
    unnamed x141, local copies, waits for them, and re-layouts  37.2 us
    dot_general x6, matrix products, contract_cols(): lax.dot_general(left_mat, right_mat, (((1,), (1,)), ((), ())), preferred_...  29.7 us
    dot_general x6, matrix products, multiply(): return jnp.dot(left_mat, right_mat, preferred_element_type=jnp.float32)  19.8 us
  transfers between devices with their start and end apart: 4, of which 4 were waited for; matrix products, arithmetic and copies ran while one was open for 10% of the time, Pallas kernels for 0%

profile of v1, /device:TPU:0, one launch (start us, length us, event | category | flops | bytes accessed | tf_op | source)
XLA Modules:
  0.0 959.8 jit_solution(933450291314227638)
XLA Ops:
  14.9 5.2 copy_convert_fusion
  20.8 5.0 reshape.315
  39.9 4.0 fusion.9
  60.7 4.2 copy.58
  68.5 150.8 %all-gather.3.cloned.1.call-done = f32[8256,768]{1,0:T(8,128)} async-done(((f32[2064,768]{1,0:T(8,128)}), f32[8256,768]{1,0:T(8,128)}) %all-gather.3.cloned.1.call-update) | async-done | bytes 25362448 | tf_op jit(solution)/shard_map/all_gather | solution.py:96
  219.3 12.5 %reduce_sum.190 = f32[2064,768]{1,0:T(8,128)} reduce(f32[4,2064,768]{2,1,0:T(8,128)} %bitcast.73, f32[]{:T(128)} %constant.39.clone.1), dimensions={0}, to_apply=%region_4.5 | reduce | flops 4755456 | bytes 31703044 | tf_op jit(solution)/shard_map/reduce_sum | solution.py:96
  231.8 5.0 reduce_sum.191
  236.9 7.8 add_convert_fusion
  248.5 7.3 add_convert_fusion.3
  258.9 18.1 %convert_reduce_fusion.1 = (f32[768]{0:T(1024)S(1)}, bf16[2064,768]{1,0:T(8,128)(2,1)S(1)}, f32[2064,768]{1,0:T(8,128)}) fusion(f32[2064,768]{1,0:T(8,128)S(1)} %convolution_add_fusion, bf16[2064,768]{1,0:T(8,128)(2,1)S(1)} %copy-done.8, bf16[768,768]{1,0:T(8,128)(2,1)S(1)} %copy-done), kind=kOutput, calls=%fused_computation.16 | convolution fusion | flops 2552093952 | bytes 20204544 | tf_op jit(solution)/shard_map/dot_general | solution.py:33
  278.6 4.6 fusion.36
  283.7 5.5 multiply_convert_fusion.1
  290.9 4.6 fusion.35
  295.4 108.5 %all-reduce.7.cloned.1.call-done = f32[2064,768]{1,0:T(8,128)} async-done(((f32[2064,768]{1,0:T(8,128)}), f32[2064,768]{1,0:T(8,128)}) %all-reduce.7.cloned.1.call-update) | async-done | bytes 6340624 | tf_op jit(solution)/shard_map/psum | solution.py:113
  404.0 5.9 multiply_reduce_fusion.4
  409.9 6.8 fusion.33
  423.6 6.8 convert_reduce_fusion.3
  430.4 7.6 multiply_reduce_fusion
  438.1 10.9 %multiply_convert_fusion = bf16[8,3,258,258]{2,3,1,0:T(8,128)(2,1)} fusion(f32[8,3,258,258]{2,3,1,0:T(8,128)} %get-tuple-element.92, f32[8,3,258,258]{2,3,1,0:T(8,128)} %copy-done.2, f32[8,3,258]{2,1,0:T(4,128)S(1)} %get-tuple-element.91, f32[8,3,258]{2,1,0:T(4,128)S(1)} %log_add_fusion), kind=kLoop, calls=%fused_computation | loop fusion | flops 7987680 | bytes 16024896 | tf_op jit(solution)/shard_map/convert_element_type | solution.py:135
  449.0 5.5 fusion.14
  478.5 8.5 fusion.40
  487.1 4.4 fusion.41
  501.0 197.0 %all-reduce.11.cloned.1.call-done = (f32[2064,768]{1,0:T(8,128)}, f32[2064,768]{1,0:T(8,128)}) async-done(((f32[2064,768]{1,0:T(8,128)}, f32[2064,768]{1,0:T(8,128)}), (f32[2064,768]{1,0:T(8,128)}, f32[2064,768]{1,0:T(8,128)})) %all-reduce.11.cloned.1.call-update) | async-done | bytes 12681232 | tf_op jit(solution)/shard_map/psum | solution.py:103
  698.0 7.2 add_convert_fusion.2
  709.1 4.9 copy.70
  714.0 7.1 multiply_reduce_fusion.5
  721.2 7.7 fusion.32
  728.9 7.4 add_multiply_fusion
  736.3 5.0 reshape.314
  741.3 7.8 copy.71
  749.2 40.1 %all-reduce = (f32[192]{0:T(256)}, f32[192]{0:T(256)}, f32[768]{0:T(1024)}, f32[768]{0:T(1024)}, f32[768]{0:T(1024)}, /*index=5*/f32[768]{0:T(1024)}, f32[768]{0:T(1024)}, f32[768]{0:T(1024)}, f32[768]{0:T(1024)}) all-reduce(f32[192]{0:T(256)S(1)} %reduce_sum.231, ...), channel_id=1, replica_groups=mesh['dp'=8,'tensor'=4] {'dp'}, use_global_device_ids=true, to_apply=%region_20.21 | all-reduce | flops 5760 | bytes 46080 | tf_op jit(solution)/shard_map/psum | solution.py:170
  789.3 152.8 %all-reduce.9.cloned.1.call-done = (f32[768,192]{0,1:T(8,128)}, f32[768,192]{0,1:T(8,128)}, f32[768,192]{0,1:T(8,128)}, f32[192,768]{1,0:T(8,128)}, f32[768,768]{1,0:T(8,128)}, /*index=5*/f32[768,768]{1,0:T(8,128)}) async-done(((f32[768,192]{0,1:T(8,128)}, f32[768,192]{0,1:T(8,128)}, f32[768,192]{0,1:T(8,128)}, f32[192,768]{1,0:T(8,128)}, f32[768,768]{1,0:T(8,128)}, /*index=5*/f32[768,768]{1,0:T(8,128)}), ...) | async-done | bytes 7077904 | tf_op jit(solution)/shard_map/psum | solution.py:170
  (205 shorter events, 108.1 us)
Async XLA Ops:
  7.2 251.4 %copy-start = (bf16[768,768]{1,0:T(8,128)(2,1)S(1)}, bf16[768,768]{1,0:T(8,128)(2,1)}, u32[]{:S(2)}) copy-start(bf16[768,768]{1,0:T(8,128)(2,1)} %param.30) | copy-start | bytes 3538948
  7.2 212.1 %all-gather.3.cloned.1.call-start = ((), (), s32[]{:S(2)}) async-start(), calls=%async_computation.1 | async-start | bytes 31703040 | tf_op jit(solution)/shard_map/all_gather | solution.py:96
  8.1 12.0 %copy-start.33 = (f32[8,258]{1,0:T(8,128)}, f32[8,258]{1,0:T(8,128)S(1)}, u32[]{:S(2)}) copy-start(f32[8,258]{1,0:T(8,128)S(1)} %broadcast_select_fusion) | copy-start | bytes 24772
  8.2 240.3 %copy-start.31 = (f32[2064]{0:T(1024)}, f32[2064]{0:T(1024)S(1)}, u32[]{:S(2)}) copy-start(f32[2064]{0:T(1024)S(1)} %select_n.13) | copy-start | bytes 24772
  11.3 8.8 copy-start.46
  11.4 14.4 %copy-start.42 = (f32[2064]{0:T(1024)}, f32[2064]{0:T(1024)S(1)}, u32[]{:S(2)}) copy-start(f32[2064]{0:T(1024)S(1)} %div.41) | copy-start | bytes 24772
  32.5 7.4 copy-start.37
  32.5 7.4 copy-start.62
  33.9 13.0 %copy-start.12 = (bf16[8,258,3,64]{1,0,3,2:T(8,128)(2,1)}, bf16[8,258,3,64]{1,0,3,2:T(8,128)(2,1)S(1)}, u32[]{:S(2)}) copy-start(bf16[8,258,3,64]{1,0,3,2:T(8,128)(2,1)S(1)} %reshape.310) | copy-start | bytes 2377732
  60.6 343.4 %all-reduce.7.cloned.1.call-start = ((), (), s32[]{:S(2)}) async-start(), calls=%async_computation | async-start | bytes 12681216 | tf_op jit(solution)/shard_map/psum | solution.py:113
  236.9 7.8 copy-start.3
  236.9 8.7 copy-start.5
  248.5 7.4 copy-start.59
  248.5 7.3 copy-start.60
  258.9 18.1 %copy-start.23 = (f32[2064,768]{1,0:T(8,128)}, f32[2064,768]{1,0:T(8,128)S(1)}, u32[]{:S(2)}) copy-start(f32[2064,768]{1,0:T(8,128)S(1)} %convolution_add_fusion) | copy-start | bytes 19021828
  283.3 414.7 %all-reduce.11.cloned.1.call-start = ((), (), s32[]{:S(2)}) async-start(), calls=%async_computation.3 | async-start | bytes 25362432 | tf_op jit(solution)/shard_map/psum | solution.py:103
  438.0 10.9 %copy-start.15 = (bf16[8,258,3,64]{1,0,3,2:T(8,128)(2,1)S(1)}, bf16[8,258,3,64]{1,0,3,2:T(8,128)(2,1)}, u32[]{:S(2)}) copy-start(bf16[8,258,3,64]{1,0,3,2:T(8,128)(2,1)} %copy-done.14) | copy-start | bytes 2377732
  455.9 13.0 %copy-start.38 = (bf16[768,192]{0,1:T(8,128)(2,1)S(1)}, bf16[768,192]{0,1:T(8,128)(2,1)}, u32[]{:S(2)}) copy-start(bf16[768,192]{0,1:T(8,128)(2,1)} %param.21) | copy-start | bytes 884740
  459.7 11.3 %copy-start.21 = (bf16[2064,192]{0,1:T(8,128)(2,1)}, bf16[2064,192]{0,1:T(8,128)(2,1)S(1)}, u32[]{:S(2)}) copy-start(bf16[2064,192]{0,1:T(8,128)(2,1)S(1)} %convert_element_type.157) | copy-start | bytes 2377732
  474.8 467.3 %all-reduce.9.cloned.1.call-start = ((), (), s32[]{:S(2)}) async-start(), calls=%async_computation.2 | async-start | bytes 14155776 | tf_op jit(solution)/shard_map/psum | solution.py:170
  478.5 8.5 copy-start.10
  478.5 8.5 copy-start.26
  496.7 201.3 %copy-start.58 = (f32[768]{0:T(1024)S(1)}, f32[768]{0:T(1024)}, u32[]{:S(2)}) copy-start(f32[768]{0:T(1024)} %param.31) | copy-start | bytes 9220
  705.2 8.7 copy-start.32
  705.2 8.7 copy-start.43
  705.2 8.7 copy-start.45
  705.2 8.7 copy-start.51
  709.1 12.1 %slice-start = ((s8[6340608]{0:T(1024)(128)(4,1)}), s8[4194304]{0:T(1024)(128)(4,1)S(1)}, s32[]{:S(2)}) async-start(s8[6340608]{0:T(1024)(128)(4,1)} %bitcast.71), calls=%async_computation.4 | async-start | bytes 8388608
  721.2 7.7 copy-start.11
  942.1 7.9 copy-start.30
  942.1 9.3 copy-start.29
  942.1 10.7 %copy-start.1 = (bf16[768,768]{1,0:T(8,128)(2,1)S(1)}, bf16[768,768]{1,0:T(8,128)(2,1)}, u32[]{:S(2)}) copy-start(bf16[768,768]{1,0:T(8,128)(2,1)} %param.30) | copy-start | bytes 3538948
  (38 other events, 157.2 us)
Sparse Core Ops, SparseCore 0:
  60.7 158.5 all-gather.2
  283.4 120.5 all-reduce.6
  474.9 223.0 all-reduce.10
  704.1 237.9 all-reduce.8
